TPU v7x, 512 devices: a whole 4x8x8 slice. The times are simulated.
512 devices in a mesh: gx: 32 (over z, x), gy: 16 (over y, core).
Axes of the slice: x: 4, y: 8, z: 8, core: 2. Of those that a mesh axis runs over, the one named last changes fastest.
Arguments:
- gap_load: float32 [32, 16, 384, 128], P('gx', 'gy'), may hold values from -6 to 6
- flexibility: bfloat16 [32, 16, 768, 768], P('gx', 'gy'), as said below
- schur_blocks: bfloat16 [32, 16, 768, 768], P('gx', 'gy'), as said below
- body_modes: float32 [32, 16, 3, 768], P('gx', 'gy'), may hold values from -6 to 6
- coarse_inverse: float32 [1536, 1536], P(('gx', 'gy')), as said below
- saved_search: float32 [32, 16, 16, 384], P('gx', 'gy'), may hold values from -6 to 6
- saved_images: float32 [32, 16, 16, 384], P('gx', 'gy'), may hold values from -0.0017089844 to 0.0017089844
- face_slots: int32 [32, 16, 4, 192], P('gx', 'gy'), may hold values from 0 to 767, as said below
- face_count: int32 [32, 16, 4], P('gx', 'gy'), may hold values from 0 to 192, as said below
- multiplicity: int32 [32, 16, 768], P('gx', 'gy'), may hold values from 1 to 3, as said below
Outputs:
- multipliers: float32 [32, 16, 384, 128], P('gx', 'gy')
- residual: float32 [32, 16, 384, 128], P('gx', 'gy')
Inputs may be any that keep to these rules, and one draw needn't show every extreme that they name: For k < face_count[a, b, d] the entries face_slots[a, b, d, k] are distinct slots of subdomain (a, b), except that faces that follow each other in the order up, right, down, left share one slot when both are not empty. Link k of the face between two neighbouring subdomains is entry k of both their lists (down of the upper one and up of the lower one, right of the left one and left of the right one). Entries with k >= face_count carry no meaning. face_count[a, b, 0] = face_count[a - 1, b, 1] and face_count[a, b, 2] = face_count[a, b - 1, 3]; faces on the grid's border have 0 links, inner faces between 96 and 192, and in every draw some face along each grid direction has exactly 192. multiplicity[a, b, i] is 1 plus the number of faces of (a, b) whose first face_count entries name slot i. `flexibility`: each block is symmetric. `schur_blocks`: each block is symmetric. `coarse_inverse`: Symmetric.
All inputs are finite; a program needn't handle non-finite values.
Results may differ from a plain program's by a relative error of at most 0.0015.
The roundings to bfloat16 on the way count: a program that leaves them out, or rounds other values in their place, can miss the bound.
Values sent between devices are 32-bit elements.
No kernel may reach another device: no remote copies, remote signals or barrier semaphores. Data moves between devices by JAX's collectives and lax.ppermute only.
A program may use at most 64 MiB of HBM per device.

v0:
```python
import functools
import jax
import jax.numpy as jnp
from jax import lax
from jax.sharding import Mesh
from jax.sharding import PartitionSpec as P

GX = ("gx_0", "gx_1")
GY = ("gy_0", "gy_1")
GX_GY = ("gx_0", "gx_1", "gy_0", "gy_1")
HIGHEST_MODE = lax.Precision.HIGHEST


def shifted(value, axis, steps):
    count = lax.axis_size(axis)
    initial, last = (max(0, -steps), min(count, count - steps))
    return lax.ppermute(value, axis, [(source, source + steps) for source in range(initial, last)])


def over_axes(x, axes):
    return functools.reduce(lax.psum, axes, x)


def place_parts(
    down_values, right_values, from_above, from_left, slot_table, face_valid, slot_total
):
    load_cases = down_values.shape[1]
    signed_parts = (
        jnp.stack([-from_above, down_values, -from_left, right_values], axis=0)
        * face_valid[:, :, None]
    )
    empty = jnp.zeros((slot_total, load_cases), jnp.float32)
    return empty.at[slot_table.reshape(-1)].add(signed_parts.reshape(-1, load_cases))


def place_full(full_links, slot_table, face_valid, slot_total):
    return place_parts(
        full_links[1],
        full_links[3],
        full_links[0],
        full_links[2],
        slot_table,
        face_valid,
        slot_total,
    )


def gain_copies(link_values, face_width):
    down_values = link_values[:face_width]
    right_values = link_values[face_width:]
    upper_copy = shifted(down_values, GX, 1)
    left_copy = shifted(right_values, GY, 1)
    return jnp.stack([upper_copy, down_values, left_copy, right_values], axis=0)


def own_links(full_links):
    return jnp.concatenate([full_links[1], full_links[3]], axis=0)


def jumps_full(slot_values, slot_table, face_valid):
    face_width = slot_table.shape[1]
    picked = jnp.take(slot_values, slot_table.reshape(-1), axis=0).reshape(
        4, face_width, slot_values.shape[1]
    )
    below_values = shifted(picked[0], GX, -1)
    right_values = shifted(picked[2], GY, -1)
    above_values = shifted(picked[1], GX, 1)
    left_values = shifted(picked[3], GY, 1)
    down_part = (picked[1] - below_values) * face_valid[1][:, None]
    right_part = (picked[3] - right_values) * face_valid[3][:, None]
    upper_part = (above_values - picked[0]) * face_valid[0][:, None]
    left_part = (left_values - picked[2]) * face_valid[2][:, None]
    return jnp.stack([upper_part, down_part, left_part, right_part], axis=0)


def late_dots(energy_part, intersect_part):
    return (over_axes(energy_part, GX_GY), over_axes(intersect_part, GX_GY))


def curvature_sum(curvature_part):
    return over_axes(curvature_part, GX_GY)


def per_device(
    gap_load,
    flexibility,
    schur_blocks,
    body_modes,
    coarse_inverse,
    saved_search,
    saved_images,
    face_slots,
    face_count,
    multiplicity,
):
    local_flex = flexibility[0, 0]
    local_schur = schur_blocks[0, 0]
    rigid_modes = body_modes[0, 0]
    slot_table = face_slots[0, 0]
    face_width = slot_table.shape[1]
    slot_total = rigid_modes.shape[1]
    face_valid = (jnp.arange(face_width)[None, :] < face_count[0, 0][:, None]).astype(jnp.float32)
    link_valid = jnp.concatenate([face_valid[1], face_valid[3]], axis=0)
    weights = 1.0 / multiplicity[0, 0].astype(jnp.float32)
    residual = gap_load[0, 0] * link_valid[:, None]
    kept_search = saved_search[0, 0] * link_valid[None, :]
    kept_images = saved_images[0, 0] * link_valid[None, :]
    residual_full = gain_copies(residual, face_width)
    search_full_kept = gain_copies(kept_search.T, face_width)
    weighted = (
        weights[:, None] * place_full(residual_full, slot_table, face_valid, slot_total)
    ).astype(jnp.bfloat16)
    smoothed = jnp.dot(local_schur, weighted, preferred_element_type=jnp.float32)
    precond_full = jumps_full(weights[:, None] * smoothed, slot_table, face_valid)
    precond = own_links(precond_full)
    energy_part = jnp.sum(own_links(residual_full) * precond, axis=0)
    coarse_in = jnp.dot(
        rigid_modes,
        place_full(precond_full, slot_table, face_valid, slot_total),
        precision=HIGHEST_MODE,
    )
    coarse_out = jnp.dot(
        coarse_inverse, lax.all_gather(coarse_in, GX_GY, axis=0, tiled=True), precision=HIGHEST_MODE
    )
    projected_full = precond_full - jumps_full(
        jnp.dot(rigid_modes.T, coarse_out, precision=HIGHEST_MODE), slot_table, face_valid
    )
    intersect_part = jnp.dot(kept_images, own_links(projected_full), precision=HIGHEST_MODE)
    energy, intersect = late_dots(energy_part, intersect_part)
    search_full = projected_full - jnp.einsum(
        "dfj,jc->dfc", search_full_kept, intersect, precision=HIGHEST_MODE
    )
    lifted = place_full(search_full, slot_table, face_valid, slot_total).astype(jnp.bfloat16)
    applied_full = jumps_full(
        jnp.dot(local_flex, lifted, preferred_element_type=jnp.float32), slot_table, face_valid
    )
    search = own_links(search_full)
    curvature = curvature_sum(jnp.sum(search * own_links(applied_full), axis=0))
    step_size = energy / curvature
    multipliers = step_size * search
    residual_full = residual_full - step_size * applied_full
    residual = own_links(residual_full)
    return (multipliers[None, None], residual[None, None])


def solution(mesh):
    split = Mesh(mesh.devices.reshape(8, 4, 8, 2), ("gx_0", "gx_1", "gy_0", "gy_1"))
    placed = (
        P(GX, GY, None, None),
        P(GX, GY, None, None),
        P(GX, GY, None, None),
        P(GX, GY, None, None),
        P(GX_GY, None),
        P(GX, GY, None, None),
        P(GX, GY, None, None),
        P(GX, GY, None, None),
        P(GX, GY, None),
        P(GX, GY, None),
    )
    return jax.shard_map(
        per_device,
        mesh=split,
        in_specs=placed,
        out_specs=(P(GX, GY, None, None), P(GX, GY, None, None)),
        check_vma=False,
    )
```

profile of v0, /device:TPU:1, one launch (start us, length us, event | category | flops | bytes accessed | tf_op | source)
XLA Modules:
  0.0 272.1 jit_solution(19171111291158714)
XLA Ops:
  2.7 4.6 %collective-permute-start.1 = (f32[192,128]{1,0:T(8,128)S(1)}, f32[192,128]{1,0:T(8,128)S(1)}, u32[]{:S(2)}, u32[]{:S(2)}) collective-permute-start(f32[192,128]{1,0:T(8,128)S(1)} %get-tuple-element.54), channel_id=1, source_target_pairs={{0,1},{1,2},{2,3},{3,4},{4,5},{5,6},{6,7},{7,8},{8,9},{9,10},{10,1... | collective-permute-start | bytes 294920 | tf_op jit(solution)/shard_map/ppermute | solution.py:17
  7.3 3.1 %collective-permute-start = (f32[192,128]{1,0:T(8,128)S(1)}, f32[192,128]{1,0:T(8,128)S(1)}, u32[]{:S(2)}, u32[]{:S(2)}) collective-permute-start(f32[192,128]{1,0:T(8,128)S(1)} %get-tuple-element.51), channel_id=1, source_target_pairs={{0,16},{16,32},{32,48},{48,64},{64,80},{80,96},{96,112},{112,128},... | collective-permute-start | bytes 294920 | tf_op jit(solution)/shard_map/ppermute | solution.py:17
  13.6 6.6 %scatter_custom_fusion = f32[768,128]{1,0:T(8,128)S(1)} fusion(s32[768]{0:T(1024)S(1)} %fusion.40, f32[768,128]{1,0:T(8,128)S(1)} %bitcast_multiply_fusion.2, f32[]{:T(128)} %constant.2.clone.1), kind=kCustom, calls=%fused_computation.53 | custom fusion | flops 98304 | bytes 393220 | tf_op jit(solution)/shard_map/scatter-add | solution.py:33
  22.9 3.0 %collective-permute-start.4 = (f32[192,128]{1,0:T(8,128)S(1)}, f32[192,128]{1,0:T(8,128)S(1)}, u32[]{:S(2)}, u32[]{:S(2)}) collective-permute-start(f32[192,128]{1,0:T(8,128)S(1)} %get-tuple-element.47), channel_id=1, source_target_pairs={{0,16},{16,32},{32,48},{48,64},{64,80},{80,96},{96,112},{112,128},... | collective-permute-start | bytes 294920 | tf_op jit(solution)/shard_map/ppermute | solution.py:17
  25.9 3.4 %collective-permute-start.5 = (f32[192,128]{1,0:T(8,128)S(1)}, f32[192,128]{1,0:T(8,128)S(1)}, u32[]{:S(2)}, u32[]{:S(2)}) collective-permute-start(f32[192,128]{1,0:T(8,128)S(1)} %get-tuple-element.49), channel_id=1, source_target_pairs={{0,1},{1,2},{2,3},{3,4},{4,5},{5,6},{6,7},{7,8},{8,9},{9,10},{10,1... | collective-permute-start | bytes 294920 | tf_op jit(solution)/shard_map/ppermute | solution.py:17
  30.6 2.5 collective-permute-start.3
  37.6 6.6 %scatter_custom_fusion.1 = f32[768,128]{1,0:T(8,128)S(1)} fusion(s32[768]{0:T(1024)S(1)} %fusion.40, f32[768,128]{1,0:T(8,128)S(1)} %bitcast_multiply_fusion.1, f32[]{:T(128)} %constant.2.clone.1), kind=kCustom, calls=%fused_computation.51 | custom fusion | flops 98304 | bytes 393220 | tf_op jit(solution)/shard_map/scatter-add | solution.py:33
  44.5 85.6 %all-gather = f32[512,3,128]{2,1,0:T(4,128)S(1)} all-gather(f32[1,3,128]{2,1,0:T(4,128)S(1)} %convolution_bitcast_fusion.2), channel_id=1, replica_groups=mesh['gx_0'=8,'gx_1'=4,'gy_0'=8,'gy_1'=2] {'gx_0','gx_1','gy_0','gy_1'}, dimensions={0}, use_global_device_ids=true | all-gather | bytes 787968 | tf_op jit(solution)/shard_map/all_gather | solution.py:123
  134.4 2.8 %collective-permute-start.6 = (f32[192,128]{1,0:T(8,128)S(1)}, f32[192,128]{1,0:T(8,128)S(1)}, u32[]{:S(2)}, u32[]{:S(2)}) collective-permute-start(f32[192,128]{1,0:T(8,128)S(1)} %get-tuple-element.39), channel_id=1, source_target_pairs={{0,16},{16,32},{32,48},{48,64},{64,80},{80,96},{96,112},{112,128},... | collective-permute-start | bytes 294920 | tf_op jit(solution)/shard_map/ppermute | solution.py:17
  138.5 2.3 collective-permute-start.9
  140.8 3.2 %collective-permute-start.8 = (f32[192,128]{1,0:T(8,128)S(1)}, f32[192,128]{1,0:T(8,128)S(1)}, u32[]{:S(2)}, u32[]{:S(2)}) collective-permute-start(f32[192,128]{1,0:T(8,128)S(1)} %get-tuple-element.41), channel_id=1, source_target_pairs={{0,1},{1,2},{2,3},{3,4},{4,5},{5,6},{6,7},{7,8},{8,9},{9,10},{10,1... | collective-permute-start | bytes 294920 | tf_op jit(solution)/shard_map/ppermute | solution.py:17
  144.1 1.9 collective-permute-start.11
  146.1 4.0 %collective-permute-start.10 = (f32[192,16]{0,1:T(8,128)S(1)}, f32[192,16]{0,1:T(8,128)S(1)}, u32[]{:S(2)}, u32[]{:S(2)}) collective-permute-start(f32[192,16]{0,1:T(8,128)S(1)} %get-tuple-element.55), channel_id=1, source_target_pairs={{0,16},{16,32},{32,48},{48,64},{64,80},{80,96},{96,112},{112,128},... | collective-permute-start | bytes 36872 | tf_op jit(solution)/shard_map/ppermute | solution.py:17
  150.7 14.6 %psum.88 = f32[16,128]{1,0:T(8,128)S(1)} all-reduce(f32[16,128]{1,0:T(8,128)S(1)} %fusion.10), channel_id=1, replica_groups=mesh['gx_0'=8,'gx_1'=4,'gy_0'=8,'gy_1'=2] {'gx_0'}, use_global_device_ids=true, to_apply=%region_7.9 | all-reduce | flops 2048 | bytes 16384 | tf_op jit(solution)/shard_map/psum | solution.py:21
  165.2 10.0 %psum.89 = f32[16,128]{1,0:T(8,128)S(1)} all-reduce(f32[16,128]{1,0:T(8,128)S(1)} %psum.88), channel_id=1, replica_groups=mesh['gx_0'=8,'gx_1'=4,'gy_0'=8,'gy_1'=2] {'gx_1'}, use_global_device_ids=true, to_apply=%region_8.10 | all-reduce | flops 2048 | bytes 16384 | tf_op jit(solution)/shard_map/psum | solution.py:21
  175.2 13.5 %psum.90 = f32[16,128]{1,0:T(8,128)S(1)} all-reduce(f32[16,128]{1,0:T(8,128)S(1)} %psum.89), channel_id=1, replica_groups=mesh['gx_0'=8,'gx_1'=4,'gy_0'=8,'gy_1'=2] {'gy_0'}, use_global_device_ids=true, to_apply=%region_9.11 | all-reduce | flops 2048 | bytes 16384 | tf_op jit(solution)/shard_map/psum | solution.py:21
  188.7 11.6 %psum.91 = f32[16,128]{1,0:T(8,128)S(1)} all-reduce(f32[16,128]{1,0:T(8,128)S(1)} %psum.90), channel_id=1, replica_groups=mesh['gx_0'=8,'gx_1'=4,'gy_0'=8,'gy_1'=2] {'gy_1'}, use_global_device_ids=true, to_apply=%region_10.12 | all-reduce | flops 2048 | bytes 16384 | tf_op jit(solution)/shard_map/psum | solution.py:21
  202.1 6.9 %scatter_custom_fusion.2 = f32[768,128]{1,0:T(8,128)S(1)} fusion(s32[768]{0:T(1024)} %copy-done.31, f32[768,128]{1,0:T(8,128)S(1)} %bitcast_multiply_fusion, f32[]{:T(128)} %constant.2.clone.1), kind=kCustom, calls=%fused_computation.49 | custom fusion | flops 98304 | bytes 393728 | tf_op jit(solution)/shard_map/scatter-add | solution.py:33
  214.3 2.4 collective-permute-start.13
  216.8 3.1 %collective-permute-start.15 = (f32[192,128]{1,0:T(8,128)S(1)}, f32[192,128]{1,0:T(8,128)S(1)}, u32[]{:S(2)}, u32[]{:S(2)}) collective-permute-start(f32[192,128]{1,0:T(8,128)S(1)} %get-tuple-element.23), channel_id=1, source_target_pairs={{0,1},{1,2},{2,3},{3,4},{4,5},{5,6},{6,7},{7,8},{8,9},{9,10},{10,1... | collective-permute-start | bytes 294920 | tf_op jit(solution)/shard_map/ppermute | solution.py:17
  221.8 16.6 %all-reduce.1 = (f32[128]{0:T(128)S(1)}, f32[128]{0:T(128)S(1)}) all-reduce(f32[128]{0:T(128)S(1)} %fusion.9, f32[128]{0:T(128)S(1)} %fusion.14), channel_id=1, replica_groups=mesh['gx_0'=8,'gx_1'=4,'gy_0'=8,'gy_1'=2] {'gx_0'}, use_global_device_ids=true, to_apply=%region_2.4 | all-reduce | flops 256 | bytes 2048 | tf_op jit(solution)/shard_map/psum | solution.py:21
  238.5 6.3 %all-reduce.2 = (f32[128]{0:T(128)S(1)}, f32[128]{0:T(128)S(1)}) all-reduce(f32[128]{0:T(128)S(1)} %get-tuple-element.5, f32[128]{0:T(128)S(1)} %get-tuple-element.6), channel_id=1, replica_groups=mesh['gx_0'=8,'gx_1'=4,'gy_0'=8,'gy_1'=2] {'gx_1'}, use_global_device_ids=true, to_apply=%region_3.5 | all-reduce | flops 256 | bytes 2048 | tf_op jit(solution)/shard_map/psum | solution.py:21
  244.7 12.4 %all-reduce = (f32[128]{0:T(128)S(1)}, f32[128]{0:T(128)S(1)}) all-reduce(f32[128]{0:T(128)S(1)} %get-tuple-element.7, f32[128]{0:T(128)S(1)} %get-tuple-element.8), channel_id=1, replica_groups=mesh['gx_0'=8,'gx_1'=4,'gy_0'=8,'gy_1'=2] {'gy_0'}, use_global_device_ids=true, to_apply=%region_4.6 | all-reduce | flops 256 | bytes 2048 | tf_op jit(solution)/shard_map/psum | solution.py:21
  257.1 13.5 %all-reduce.3 = (f32[128]{0:T(128)S(1)}, f32[128]{0:T(128)S(1)}) all-reduce(f32[128]{0:T(128)S(1)} %get-tuple-element.3, f32[128]{0:T(128)S(1)} %get-tuple-element.4), channel_id=1, replica_groups=mesh['gx_0'=8,'gx_1'=4,'gy_0'=8,'gy_1'=2] {'gy_1'}, use_global_device_ids=true, to_apply=%region_5.7 | all-reduce | flops 256 | bytes 2048 | tf_op jit(solution)/shard_map/psum | solution.py:21
  (140 shorter events, 30.0 us)
Async XLA Ops:
  1.5 35.1 %copy-start.17 = (f32[1,192]{1,0:T(1,128)}, f32[1,192]{1,0:T(1,128)S(1)}, u32[]{:S(2)}) copy-start(f32[1,192]{1,0:T(1,128)S(1)} %get-tuple-element.61) | copy-start | bytes 2308
  1.5 35.1 %copy-start.19 = (f32[1,192]{1,0:T(1,128)}, f32[1,192]{1,0:T(1,128)S(1)}, u32[]{:S(2)}) copy-start(f32[1,192]{1,0:T(1,128)S(1)} %get-tuple-element.62) | copy-start | bytes 2308
  1.6 148.8 %copy-start.15 = (f32[384]{0:T(512)}, f32[384]{0:T(512)S(1)}, u32[]{:S(2)}) copy-start(f32[384]{0:T(512)S(1)} %pad_maximum_fusion.9) | copy-start | bytes 4612
  2.7 10.1 %collective-permute-start.1 = (f32[192,128]{1,0:T(8,128)S(1)}, f32[192,128]{1,0:T(8,128)S(1)}, u32[]{:S(2)}, u32[]{:S(2)}) collective-permute-start(f32[192,128]{1,0:T(8,128)S(1)} %get-tuple-element.54), channel_id=1, source_target_pairs={{0,1},{1,2},{2,3},{3,4},{4,5},{5,6},{6,7},{7,8},{8,9},{9,10},{10,1... | collective-permute-start | bytes 294920 | tf_op jit(solution)/shard_map/ppermute | solution.py:17
  7.3 5.6 %collective-permute-start = (f32[192,128]{1,0:T(8,128)S(1)}, f32[192,128]{1,0:T(8,128)S(1)}, u32[]{:S(2)}, u32[]{:S(2)}) collective-permute-start(f32[192,128]{1,0:T(8,128)S(1)} %get-tuple-element.51), channel_id=1, source_target_pairs={{0,16},{16,32},{32,48},{48,64},{64,80},{80,96},{96,112},{112,128},... | collective-permute-start | bytes 294920 | tf_op jit(solution)/shard_map/ppermute | solution.py:17
  12.8 119.7 %copy-start.13 = (s32[1024]{0:T(1024)}, s32[1024]{0:T(1024)S(1)}, u32[]{:S(2)}) copy-start(s32[1024]{0:T(1024)S(1)} %pad_clamp_fusion) | copy-start | bytes 12292
  22.9 10.3 %collective-permute-start.4 = (f32[192,128]{1,0:T(8,128)S(1)}, f32[192,128]{1,0:T(8,128)S(1)}, u32[]{:S(2)}, u32[]{:S(2)}) collective-permute-start(f32[192,128]{1,0:T(8,128)S(1)} %get-tuple-element.47), channel_id=1, source_target_pairs={{0,16},{16,32},{32,48},{48,64},{64,80},{80,96},{96,112},{112,128},... | collective-permute-start | bytes 294920 | tf_op jit(solution)/shard_map/ppermute | solution.py:17
  25.9 7.3 %collective-permute-start.5 = (f32[192,128]{1,0:T(8,128)S(1)}, f32[192,128]{1,0:T(8,128)S(1)}, u32[]{:S(2)}, u32[]{:S(2)}) collective-permute-start(f32[192,128]{1,0:T(8,128)S(1)} %get-tuple-element.49), channel_id=1, source_target_pairs={{0,1},{1,2},{2,3},{3,4},{4,5},{5,6},{6,7},{7,8},{8,9},{9,10},{10,1... | collective-permute-start | bytes 294920 | tf_op jit(solution)/shard_map/ppermute | solution.py:17
  29.3 5.4 %collective-permute-start.2 = (f32[192,128]{1,0:T(8,128)S(1)}, f32[192,128]{1,0:T(8,128)S(1)}, u32[]{:S(2)}, u32[]{:S(2)}) collective-permute-start(f32[192,128]{1,0:T(8,128)S(1)} %get-tuple-element.50), channel_id=1, source_target_pairs={{16,0},{32,16},{48,32},{64,48},{80,64},{96,80},{112,96},{128,112},... | collective-permute-start | bytes 294920 | tf_op jit(solution)/shard_map/ppermute | solution.py:17
  30.6 5.9 %collective-permute-start.3 = (f32[192,128]{1,0:T(8,128)S(1)}, f32[192,128]{1,0:T(8,128)S(1)}, u32[]{:S(2)}, u32[]{:S(2)}) collective-permute-start(f32[192,128]{1,0:T(8,128)S(1)} %get-tuple-element.48), channel_id=1, source_target_pairs={{1,0},{2,1},{3,2},{4,3},{5,4},{6,5},{7,6},{8,7},{9,8},{10,9},{11,1... | collective-permute-start | bytes 294920 | tf_op jit(solution)/shard_map/ppermute | solution.py:17
  134.4 11.7 %collective-permute-start.6 = (f32[192,128]{1,0:T(8,128)S(1)}, f32[192,128]{1,0:T(8,128)S(1)}, u32[]{:S(2)}, u32[]{:S(2)}) collective-permute-start(f32[192,128]{1,0:T(8,128)S(1)} %get-tuple-element.39), channel_id=1, source_target_pairs={{0,16},{16,32},{32,48},{48,64},{64,80},{80,96},{96,112},{112,128},... | collective-permute-start | bytes 294920 | tf_op jit(solution)/shard_map/ppermute | solution.py:17
  137.2 12.9 %collective-permute-start.7 = (f32[192,128]{1,0:T(8,128)S(1)}, f32[192,128]{1,0:T(8,128)S(1)}, u32[]{:S(2)}, u32[]{:S(2)}) collective-permute-start(f32[192,128]{1,0:T(8,128)S(1)} %get-tuple-element.42), channel_id=1, source_target_pairs={{16,0},{32,16},{48,32},{64,48},{80,64},{96,80},{112,96},{128,112},... | collective-permute-start | bytes 294920 | tf_op jit(solution)/shard_map/ppermute | solution.py:17
  138.5 11.6 %collective-permute-start.9 = (f32[192,128]{1,0:T(8,128)S(1)}, f32[192,128]{1,0:T(8,128)S(1)}, u32[]{:S(2)}, u32[]{:S(2)}) collective-permute-start(f32[192,128]{1,0:T(8,128)S(1)} %get-tuple-element.40), channel_id=1, source_target_pairs={{1,0},{2,1},{3,2},{4,3},{5,4},{6,5},{7,6},{8,7},{9,8},{10,9},{11,1... | collective-permute-start | bytes 294920 | tf_op jit(solution)/shard_map/ppermute | solution.py:17
  140.8 9.3 %collective-permute-start.8 = (f32[192,128]{1,0:T(8,128)S(1)}, f32[192,128]{1,0:T(8,128)S(1)}, u32[]{:S(2)}, u32[]{:S(2)}) collective-permute-start(f32[192,128]{1,0:T(8,128)S(1)} %get-tuple-element.41), channel_id=1, source_target_pairs={{0,1},{1,2},{2,3},{3,4},{4,5},{5,6},{6,7},{7,8},{8,9},{9,10},{10,1... | collective-permute-start | bytes 294920 | tf_op jit(solution)/shard_map/ppermute | solution.py:17
  144.1 56.2 %collective-permute-start.11 = (f32[192,16]{0,1:T(8,128)S(1)}, f32[192,16]{0,1:T(8,128)S(1)}, u32[]{:S(2)}, u32[]{:S(2)}) collective-permute-start(f32[192,16]{0,1:T(8,128)S(1)} %get-tuple-element.58), channel_id=1, source_target_pairs={{0,1},{1,2},{2,3},{3,4},{4,5},{5,6},{6,7},{7,8},{8,9},{9,10},{10,1... | collective-permute-start | bytes 36872 | tf_op jit(solution)/shard_map/ppermute | solution.py:17
  146.1 54.2 %collective-permute-start.10 = (f32[192,16]{0,1:T(8,128)S(1)}, f32[192,16]{0,1:T(8,128)S(1)}, u32[]{:S(2)}, u32[]{:S(2)}) collective-permute-start(f32[192,16]{0,1:T(8,128)S(1)} %get-tuple-element.55), channel_id=1, source_target_pairs={{0,16},{16,32},{32,48},{48,64},{64,80},{80,96},{96,112},{112,128},... | collective-permute-start | bytes 36872 | tf_op jit(solution)/shard_map/ppermute | solution.py:17
  211.6 59.0 %copy-start.4 = (f32[192,128]{1,0:T(8,128)S(1)}, f32[192,128]{1,0:T(8,128)}, u32[]{:S(2)}) copy-start(f32[192,128]{1,0:T(8,128)} %copy-done.3) | copy-start | bytes 294916
  211.6 59.0 %copy-start.6 = (f32[192,128]{1,0:T(8,128)S(1)}, f32[192,128]{1,0:T(8,128)}, u32[]{:S(2)}) copy-start(f32[192,128]{1,0:T(8,128)} %copy-done.5) | copy-start | bytes 294916
  211.6 8.5 %collective-permute-start.14 = (f32[192,128]{1,0:T(8,128)S(1)}, f32[192,128]{1,0:T(8,128)S(1)}, u32[]{:S(2)}, u32[]{:S(2)}) collective-permute-start(f32[192,128]{1,0:T(8,128)S(1)} %get-tuple-element.21), channel_id=1, source_target_pairs={{0,16},{16,32},{32,48},{48,64},{64,80},{80,96},{96,112},{112,128},... | collective-permute-start | bytes 294920 | tf_op jit(solution)/shard_map/ppermute | solution.py:17
  213.0 7.0 %collective-permute-start.12 = (f32[192,128]{1,0:T(8,128)S(1)}, f32[192,128]{1,0:T(8,128)S(1)}, u32[]{:S(2)}, u32[]{:S(2)}) collective-permute-start(f32[192,128]{1,0:T(8,128)S(1)} %get-tuple-element.24), channel_id=1, source_target_pairs={{16,0},{32,16},{48,32},{64,48},{80,64},{96,80},{112,96},{128,112},... | collective-permute-start | bytes 294920 | tf_op jit(solution)/shard_map/ppermute | solution.py:17
  214.3 5.9 %collective-permute-start.13 = (f32[192,128]{1,0:T(8,128)S(1)}, f32[192,128]{1,0:T(8,128)S(1)}, u32[]{:S(2)}, u32[]{:S(2)}) collective-permute-start(f32[192,128]{1,0:T(8,128)S(1)} %get-tuple-element.22), channel_id=1, source_target_pairs={{1,0},{2,1},{3,2},{4,3},{5,4},{6,5},{7,6},{8,7},{9,8},{10,9},{11,1... | collective-permute-start | bytes 294920 | tf_op jit(solution)/shard_map/ppermute | solution.py:17
  216.8 4.7 %collective-permute-start.15 = (f32[192,128]{1,0:T(8,128)S(1)}, f32[192,128]{1,0:T(8,128)S(1)}, u32[]{:S(2)}, u32[]{:S(2)}) collective-permute-start(f32[192,128]{1,0:T(8,128)S(1)} %get-tuple-element.23), channel_id=1, source_target_pairs={{0,1},{1,2},{2,3},{3,4},{4,5},{5,6},{6,7},{7,8},{8,9},{9,10},{10,1... | collective-permute-start | bytes 294920 | tf_op jit(solution)/shard_map/ppermute | solution.py:17
  221.7 49.0 %copy-start.7 = (f32[1,1,192,128]{3,2,1,0:T(8,128)S(1)}, f32[1,1,192,128]{3,2,1,0:T(8,128)}, u32[]{:S(2)}) copy-start(f32[1,1,192,128]{3,2,1,0:T(8,128)} %get-tuple-element.27) | copy-start | bytes 294916
  221.7 49.0 %copy-start.8 = (f32[1,1,192,128]{3,2,1,0:T(8,128)S(1)}, f32[1,1,192,128]{3,2,1,0:T(8,128)}, u32[]{:S(2)}) copy-start(f32[1,1,192,128]{3,2,1,0:T(8,128)} %get-tuple-element.29) | copy-start | bytes 294916
  (24 other events, 296.4 us)
where the time goes:
time: 273 us; the launch traced here: 272 us
  blocking collectives  184 us (67%)
  starting transfers between devices  41.7 us (15%)
  other arithmetic  27.5 us (10%)
  local copies, waits for them, and re-layouts  8.11 us (3%)
  waiting for transfers between devices  4.85 us (2%)
  matrix products  4.32 us (2%)
    psum x8, blocking collectives, over_axes(): return functools.reduce(lax.psum, axes, x)  98.4 us
    all_gather x1, blocking collectives, per_device(): lax.all_gather(coarse_in, GX_GY, axis=0, tiled=True)  85.6 us
    ppermute x16, starting transfers between devices, shifted(): lax.ppermute(value, axis, [(source, source + steps) for source in range(i...  41.7 us
    scatter-add x3, other arithmetic, place_parts(): empty.at[slot_table.reshape(-1)].add(signed_parts.reshape(-1, load_cases))  20.1 us
  transfers between devices with their start and end apart: 16, of which 4 were waited for; matrix products, arithmetic and copies ran while one was open for 1% of the time, Pallas kernels for 0%

commit v1 on v0

--- a/solution.py
+++ b/solution.py
@@ -120,7 +120,11 @@
         precision=HIGHEST_MODE,
     )
     coarse_out = jnp.dot(
-        coarse_inverse, lax.all_gather(coarse_in, GX_GY, axis=0, tiled=True), precision=HIGHEST_MODE
+        coarse_inverse,
+        jnp.concatenate(
+            lax.all_to_all(jnp.stack([coarse_in] * lax.axis_size(GX_GY)), GX_GY, 0, 0), axis=0
+        ),
+        precision=HIGHEST_MODE,
     )
     projected_full = precond_full - jumps_full(
         jnp.dot(rigid_modes.T, coarse_out, precision=HIGHEST_MODE), slot_table, face_valid

time: 273 us -> 245 us (0.90)
  blocking collectives: 184 us -> 94.9 us
  waiting for transfers between devices: 4.85 us -> 38.5 us
  starting transfers between devices: 41.7 us -> 67.1 us
    all_gather x1 -> x0, blocking collectives: 85.6 us -> none  [per_device(): lax.all_gather(coarse_in, GX_GY, axis=0, tiled=True)]
    all_to_all x0 -> x1, waiting for transfers between devices: none -> 33.6 us  [per_device(): lax.all_to_all(jnp.stack([coarse_in] * lax.axis_size(GX_GY)), GX_GY, 0, 0)]
    all_to_all x0 -> x1, starting transfers between devices: none -> 26.1 us  [per_device(): lax.all_to_all(jnp.stack([coarse_in] * lax.axis_size(GX_GY)), GX_GY, 0, 0)]
    psum x8, blocking collectives: 98.4 us -> 94.9 us  [over_axes(): return functools.reduce(lax.psum, axes, x)]
  transfers between devices with their start and end apart: 16 -> 17, of which waited for: 4 -> 5; matrix products, arithmetic and copies ran while one was open for 1% -> 1% of each run, Pallas kernels for 0% -> 0%
where the time goes in v1:
time: 245 us; the launch traced here: 244 us
  blocking collectives  94.9 us (39%)
  starting transfers between devices  67.1 us (27%)
  waiting for transfers between devices  38.5 us (16%)
  other arithmetic  27.5 us (11%)
  local copies, waits for them, and re-layouts  9.26 us (4%)
  matrix products  5.1 us (2%)
    psum x8, blocking collectives, over_axes(): return functools.reduce(lax.psum, axes, x)  94.9 us
    ppermute x16, starting transfers between devices, shifted(): lax.ppermute(value, axis, [(source, source + steps) for source in range(i...  41 us
    all_to_all x1, waiting for transfers between devices, per_device(): lax.all_to_all(jnp.stack([coarse_in] * lax.axis_size(GX_GY)), GX_GY, 0, 0)  33.6 us
    all_to_all x1, starting transfers between devices, per_device(): lax.all_to_all(jnp.stack([coarse_in] * lax.axis_size(GX_GY)), GX_GY, 0, 0)  26.1 us
    scatter-add x3, other arithmetic, place_parts(): empty.at[slot_table.reshape(-1)].add(signed_parts.reshape(-1, load_cases))  20.1 us
  transfers between devices with their start and end apart: 17, of which 5 were waited for; matrix products, arithmetic and copies ran while one was open for 1% of the time, Pallas kernels for 0%

profile of v1, /device:TPU:1, one launch (start us, length us, event | category | flops | bytes accessed | tf_op | source)
XLA Modules:
  0.0 244.0 jit_solution(17737646935898276196)
XLA Ops:
  2.7 4.6 %collective-permute-start.1 = (f32[192,128]{1,0:T(8,128)S(1)}, f32[192,128]{1,0:T(8,128)S(1)}, u32[]{:S(2)}, u32[]{:S(2)}) collective-permute-start(f32[192,128]{1,0:T(8,128)S(1)} %get-tuple-element.54), channel_id=1, source_target_pairs={{0,1},{1,2},{2,3},{3,4},{4,5},{5,6},{6,7},{7,8},{8,9},{9,10},{10,1... | collective-permute-start | bytes 294920 | tf_op jit(solution)/shard_map/ppermute | solution.py:17
  7.3 3.1 %collective-permute-start = (f32[192,128]{1,0:T(8,128)S(1)}, f32[192,128]{1,0:T(8,128)S(1)}, u32[]{:S(2)}, u32[]{:S(2)}) collective-permute-start(f32[192,128]{1,0:T(8,128)S(1)} %get-tuple-element.51), channel_id=1, source_target_pairs={{0,16},{16,32},{32,48},{48,64},{64,80},{80,96},{96,112},{112,128},... | collective-permute-start | bytes 294920 | tf_op jit(solution)/shard_map/ppermute | solution.py:17
  13.7 6.6 %scatter_custom_fusion = f32[768,128]{1,0:T(8,128)S(1)} fusion(s32[768]{0:T(1024)S(1)} %fusion.40, f32[768,128]{1,0:T(8,128)S(1)} %bitcast_multiply_fusion.2, f32[]{:T(128)} %constant.2.clone.1), kind=kCustom, calls=%fused_computation.53 | custom fusion | flops 98304 | bytes 393220 | tf_op jit(solution)/shard_map/scatter-add | solution.py:33
  22.9 3.0 %collective-permute-start.4 = (f32[192,128]{1,0:T(8,128)S(1)}, f32[192,128]{1,0:T(8,128)S(1)}, u32[]{:S(2)}, u32[]{:S(2)}) collective-permute-start(f32[192,128]{1,0:T(8,128)S(1)} %get-tuple-element.47), channel_id=1, source_target_pairs={{0,16},{16,32},{32,48},{48,64},{64,80},{80,96},{96,112},{112,128},... | collective-permute-start | bytes 294920 | tf_op jit(solution)/shard_map/ppermute | solution.py:17
  25.9 3.4 %collective-permute-start.5 = (f32[192,128]{1,0:T(8,128)S(1)}, f32[192,128]{1,0:T(8,128)S(1)}, u32[]{:S(2)}, u32[]{:S(2)}) collective-permute-start(f32[192,128]{1,0:T(8,128)S(1)} %get-tuple-element.49), channel_id=1, source_target_pairs={{0,1},{1,2},{2,3},{3,4},{4,5},{5,6},{6,7},{7,8},{8,9},{9,10},{10,1... | collective-permute-start | bytes 294920 | tf_op jit(solution)/shard_map/ppermute | solution.py:17
  30.6 2.5 %collective-permute-start.3 = (f32[192,128]{1,0:T(8,128)S(1)}, f32[192,128]{1,0:T(8,128)S(1)}, u32[]{:S(2)}, u32[]{:S(2)}) collective-permute-start(f32[192,128]{1,0:T(8,128)S(1)} %get-tuple-element.48), channel_id=1, source_target_pairs={{1,0},{2,1},{3,2},{4,3},{5,4},{6,5},{7,6},{8,7},{9,8},{10,9},{11,1... | collective-permute-start | bytes 294920 | tf_op jit(solution)/shard_map/ppermute | solution.py:17
  37.6 6.6 %scatter_custom_fusion.1 = f32[768,128]{1,0:T(8,128)S(1)} fusion(s32[768]{0:T(1024)S(1)} %fusion.40, f32[768,128]{1,0:T(8,128)S(1)} %bitcast_multiply_fusion.1, f32[]{:T(128)} %constant.2.clone.1), kind=kCustom, calls=%fused_computation.51 | custom fusion | flops 98304 | bytes 393220 | tf_op jit(solution)/shard_map/scatter-add | solution.py:33
  45.7 26.1 %all-to-all-start = ((f32[512,3,128]{2,1,0:T(4,128)}), f32[512,3,128]{2,1,0:T(4,128)S(1)}, u32[]{:S(2)}, u32[]{:S(2)}) async-start(f32[512,3,128]{2,1,0:T(4,128)} %stack.87), calls=%async_computation | async-start | bytes 2097152 | tf_op jit(solution)/shard_map/all_to_all | solution.py:125
  71.8 33.6 %all-to-all-done = f32[512,3,128]{2,1,0:T(4,128)S(1)} async-done(((f32[512,3,128]{2,1,0:T(4,128)}), f32[512,3,128]{2,1,0:T(4,128)S(1)}, u32[]{:S(2)}, u32[]{:S(2)}) %all-to-all-start) | async-done | bytes 786464 | tf_op jit(solution)/shard_map/all_to_all | solution.py:125
  113.2 3.1 %collective-permute-start.9 = (f32[192,128]{1,0:T(8,128)S(1)}, f32[192,128]{1,0:T(8,128)S(1)}, u32[]{:S(2)}, u32[]{:S(2)}) collective-permute-start(f32[192,128]{1,0:T(8,128)S(1)} %get-tuple-element.40), channel_id=1, source_target_pairs={{1,0},{2,1},{3,2},{4,3},{5,4},{6,5},{7,6},{8,7},{9,8},{10,9},{11,1... | collective-permute-start | bytes 294920 | tf_op jit(solution)/shard_map/ppermute | solution.py:17
  116.3 2.5 %collective-permute-start.8 = (f32[192,128]{1,0:T(8,128)S(1)}, f32[192,128]{1,0:T(8,128)S(1)}, u32[]{:S(2)}, u32[]{:S(2)}) collective-permute-start(f32[192,128]{1,0:T(8,128)S(1)} %get-tuple-element.41), channel_id=1, source_target_pairs={{0,1},{1,2},{2,3},{3,4},{4,5},{5,6},{6,7},{7,8},{8,9},{9,10},{10,1... | collective-permute-start | bytes 294920 | tf_op jit(solution)/shard_map/ppermute | solution.py:17
  118.8 2.2 collective-permute-start.11
  121.1 4.3 %collective-permute-start.10 = (f32[192,16]{0,1:T(8,128)S(1)}, f32[192,16]{0,1:T(8,128)S(1)}, u32[]{:S(2)}, u32[]{:S(2)}) collective-permute-start(f32[192,16]{0,1:T(8,128)S(1)} %get-tuple-element.55), channel_id=1, source_target_pairs={{0,16},{16,32},{32,48},{48,64},{64,80},{80,96},{96,112},{112,128},... | collective-permute-start | bytes 36872 | tf_op jit(solution)/shard_map/ppermute | solution.py:17
  126.0 13.8 %psum.88 = f32[16,128]{1,0:T(8,128)S(1)} all-reduce(f32[16,128]{1,0:T(8,128)S(1)} %fusion.10), channel_id=1, replica_groups=mesh['gx_0'=8,'gx_1'=4,'gy_0'=8,'gy_1'=2] {'gx_0'}, use_global_device_ids=true, to_apply=%region_7.9 | all-reduce | flops 2048 | bytes 16384 | tf_op jit(solution)/shard_map/psum | solution.py:21
  139.7 9.2 %psum.89 = f32[16,128]{1,0:T(8,128)S(1)} all-reduce(f32[16,128]{1,0:T(8,128)S(1)} %psum.88), channel_id=1, replica_groups=mesh['gx_0'=8,'gx_1'=4,'gy_0'=8,'gy_1'=2] {'gx_1'}, use_global_device_ids=true, to_apply=%region_8.10 | all-reduce | flops 2048 | bytes 16384 | tf_op jit(solution)/shard_map/psum | solution.py:21
  149.0 12.4 %psum.90 = f32[16,128]{1,0:T(8,128)S(1)} all-reduce(f32[16,128]{1,0:T(8,128)S(1)} %psum.89), channel_id=1, replica_groups=mesh['gx_0'=8,'gx_1'=4,'gy_0'=8,'gy_1'=2] {'gy_0'}, use_global_device_ids=true, to_apply=%region_9.11 | all-reduce | flops 2048 | bytes 16384 | tf_op jit(solution)/shard_map/psum | solution.py:21
  161.4 11.6 %psum.91 = f32[16,128]{1,0:T(8,128)S(1)} all-reduce(f32[16,128]{1,0:T(8,128)S(1)} %psum.90), channel_id=1, replica_groups=mesh['gx_0'=8,'gx_1'=4,'gy_0'=8,'gy_1'=2] {'gy_1'}, use_global_device_ids=true, to_apply=%region_10.12 | all-reduce | flops 2048 | bytes 16384 | tf_op jit(solution)/shard_map/psum | solution.py:21
  174.7 6.9 %scatter_custom_fusion.2 = f32[768,128]{1,0:T(8,128)S(1)} fusion(s32[768]{0:T(1024)} %copy-done.31, f32[768,128]{1,0:T(8,128)S(1)} %bitcast_multiply_fusion, f32[]{:T(128)} %constant.2.clone.1), kind=kCustom, calls=%fused_computation.49 | custom fusion | flops 98304 | bytes 393728 | tf_op jit(solution)/shard_map/scatter-add | solution.py:33
  187.0 2.4 collective-permute-start.13
  189.4 3.1 %collective-permute-start.15 = (f32[192,128]{1,0:T(8,128)S(1)}, f32[192,128]{1,0:T(8,128)S(1)}, u32[]{:S(2)}, u32[]{:S(2)}) collective-permute-start(f32[192,128]{1,0:T(8,128)S(1)} %get-tuple-element.23), channel_id=1, source_target_pairs={{0,1},{1,2},{2,3},{3,4},{4,5},{5,6},{6,7},{7,8},{8,9},{9,10},{10,1... | collective-permute-start | bytes 294920 | tf_op jit(solution)/shard_map/ppermute | solution.py:17
  194.5 16.3 %all-reduce.1 = (f32[128]{0:T(128)S(1)}, f32[128]{0:T(128)S(1)}) all-reduce(f32[128]{0:T(128)S(1)} %fusion.9, f32[128]{0:T(128)S(1)} %fusion.14), channel_id=1, replica_groups=mesh['gx_0'=8,'gx_1'=4,'gy_0'=8,'gy_1'=2] {'gx_0'}, use_global_device_ids=true, to_apply=%region_2.4 | all-reduce | flops 256 | bytes 2048 | tf_op jit(solution)/shard_map/psum | solution.py:21
  210.8 6.6 %all-reduce.2 = (f32[128]{0:T(128)S(1)}, f32[128]{0:T(128)S(1)}) all-reduce(f32[128]{0:T(128)S(1)} %get-tuple-element.5, f32[128]{0:T(128)S(1)} %get-tuple-element.6), channel_id=1, replica_groups=mesh['gx_0'=8,'gx_1'=4,'gy_0'=8,'gy_1'=2] {'gx_1'}, use_global_device_ids=true, to_apply=%region_3.5 | all-reduce | flops 256 | bytes 2048 | tf_op jit(solution)/shard_map/psum | solution.py:21
  217.3 11.5 %all-reduce = (f32[128]{0:T(128)S(1)}, f32[128]{0:T(128)S(1)}) all-reduce(f32[128]{0:T(128)S(1)} %get-tuple-element.7, f32[128]{0:T(128)S(1)} %get-tuple-element.8), channel_id=1, replica_groups=mesh['gx_0'=8,'gx_1'=4,'gy_0'=8,'gy_1'=2] {'gy_0'}, use_global_device_ids=true, to_apply=%region_4.6 | all-reduce | flops 256 | bytes 2048 | tf_op jit(solution)/shard_map/psum | solution.py:21
  228.9 13.6 %all-reduce.3 = (f32[128]{0:T(128)S(1)}, f32[128]{0:T(128)S(1)}) all-reduce(f32[128]{0:T(128)S(1)} %get-tuple-element.3, f32[128]{0:T(128)S(1)} %get-tuple-element.4), channel_id=1, replica_groups=mesh['gx_0'=8,'gx_1'=4,'gy_0'=8,'gy_1'=2] {'gy_1'}, use_global_device_ids=true, to_apply=%region_5.7 | all-reduce | flops 256 | bytes 2048 | tf_op jit(solution)/shard_map/psum | solution.py:21
  (142 shorter events, 33.4 us)
Async XLA Ops:
  1.5 35.1 %copy-start.19 = (f32[1,192]{1,0:T(1,128)}, f32[1,192]{1,0:T(1,128)S(1)}, u32[]{:S(2)}) copy-start(f32[1,192]{1,0:T(1,128)S(1)} %get-tuple-element.62) | copy-start | bytes 2308
  1.6 124.2 %copy-start.15 = (f32[384]{0:T(512)}, f32[384]{0:T(512)S(1)}, u32[]{:S(2)}) copy-start(f32[384]{0:T(512)S(1)} %pad_maximum_fusion.9) | copy-start | bytes 4612
  2.7 10.1 %collective-permute-start.1 = (f32[192,128]{1,0:T(8,128)S(1)}, f32[192,128]{1,0:T(8,128)S(1)}, u32[]{:S(2)}, u32[]{:S(2)}) collective-permute-start(f32[192,128]{1,0:T(8,128)S(1)} %get-tuple-element.54), channel_id=1, source_target_pairs={{0,1},{1,2},{2,3},{3,4},{4,5},{5,6},{6,7},{7,8},{8,9},{9,10},{10,1... | collective-permute-start | bytes 294920 | tf_op jit(solution)/shard_map/ppermute | solution.py:17
  7.3 5.6 %collective-permute-start = (f32[192,128]{1,0:T(8,128)S(1)}, f32[192,128]{1,0:T(8,128)S(1)}, u32[]{:S(2)}, u32[]{:S(2)}) collective-permute-start(f32[192,128]{1,0:T(8,128)S(1)} %get-tuple-element.51), channel_id=1, source_target_pairs={{0,16},{16,32},{32,48},{48,64},{64,80},{80,96},{96,112},{112,128},... | collective-permute-start | bytes 294920 | tf_op jit(solution)/shard_map/ppermute | solution.py:17
  12.8 95.7 %copy-start.13 = (s32[1024]{0:T(1024)}, s32[1024]{0:T(1024)S(1)}, u32[]{:S(2)}) copy-start(s32[1024]{0:T(1024)S(1)} %pad_clamp_fusion) | copy-start | bytes 12292
  22.9 10.2 %collective-permute-start.4 = (f32[192,128]{1,0:T(8,128)S(1)}, f32[192,128]{1,0:T(8,128)S(1)}, u32[]{:S(2)}, u32[]{:S(2)}) collective-permute-start(f32[192,128]{1,0:T(8,128)S(1)} %get-tuple-element.47), channel_id=1, source_target_pairs={{0,16},{16,32},{32,48},{48,64},{64,80},{80,96},{96,112},{112,128},... | collective-permute-start | bytes 294920 | tf_op jit(solution)/shard_map/ppermute | solution.py:17
  25.9 7.3 %collective-permute-start.5 = (f32[192,128]{1,0:T(8,128)S(1)}, f32[192,128]{1,0:T(8,128)S(1)}, u32[]{:S(2)}, u32[]{:S(2)}) collective-permute-start(f32[192,128]{1,0:T(8,128)S(1)} %get-tuple-element.49), channel_id=1, source_target_pairs={{0,1},{1,2},{2,3},{3,4},{4,5},{5,6},{6,7},{7,8},{8,9},{9,10},{10,1... | collective-permute-start | bytes 294920 | tf_op jit(solution)/shard_map/ppermute | solution.py:17
  29.3 5.4 %collective-permute-start.2 = (f32[192,128]{1,0:T(8,128)S(1)}, f32[192,128]{1,0:T(8,128)S(1)}, u32[]{:S(2)}, u32[]{:S(2)}) collective-permute-start(f32[192,128]{1,0:T(8,128)S(1)} %get-tuple-element.50), channel_id=1, source_target_pairs={{16,0},{32,16},{48,32},{64,48},{80,64},{96,80},{112,96},{128,112},... | collective-permute-start | bytes 294920 | tf_op jit(solution)/shard_map/ppermute | solution.py:17
  30.6 5.9 %collective-permute-start.3 = (f32[192,128]{1,0:T(8,128)S(1)}, f32[192,128]{1,0:T(8,128)S(1)}, u32[]{:S(2)}, u32[]{:S(2)}) collective-permute-start(f32[192,128]{1,0:T(8,128)S(1)} %get-tuple-element.48), channel_id=1, source_target_pairs={{1,0},{2,1},{3,2},{4,3},{5,4},{6,5},{7,6},{8,7},{9,8},{10,9},{11,1... | collective-permute-start | bytes 294920 | tf_op jit(solution)/shard_map/ppermute | solution.py:17
  45.7 59.7 %all-to-all-start = ((f32[512,3,128]{2,1,0:T(4,128)}), f32[512,3,128]{2,1,0:T(4,128)S(1)}, u32[]{:S(2)}, u32[]{:S(2)}) async-start(f32[512,3,128]{2,1,0:T(4,128)} %stack.87), calls=%async_computation | async-start | bytes 2097152 | tf_op jit(solution)/shard_map/all_to_all | solution.py:125
  110.4 10.7 %collective-permute-start.6 = (f32[192,128]{1,0:T(8,128)S(1)}, f32[192,128]{1,0:T(8,128)S(1)}, u32[]{:S(2)}, u32[]{:S(2)}) collective-permute-start(f32[192,128]{1,0:T(8,128)S(1)} %get-tuple-element.39), channel_id=1, source_target_pairs={{0,16},{16,32},{32,48},{48,64},{64,80},{80,96},{96,112},{112,128},... | collective-permute-start | bytes 294920 | tf_op jit(solution)/shard_map/ppermute | solution.py:17
  111.9 13.5 %collective-permute-start.7 = (f32[192,128]{1,0:T(8,128)S(1)}, f32[192,128]{1,0:T(8,128)S(1)}, u32[]{:S(2)}, u32[]{:S(2)}) collective-permute-start(f32[192,128]{1,0:T(8,128)S(1)} %get-tuple-element.42), channel_id=1, source_target_pairs={{16,0},{32,16},{48,32},{64,48},{80,64},{96,80},{112,96},{128,112},... | collective-permute-start | bytes 294920 | tf_op jit(solution)/shard_map/ppermute | solution.py:17
  113.2 12.2 %collective-permute-start.9 = (f32[192,128]{1,0:T(8,128)S(1)}, f32[192,128]{1,0:T(8,128)S(1)}, u32[]{:S(2)}, u32[]{:S(2)}) collective-permute-start(f32[192,128]{1,0:T(8,128)S(1)} %get-tuple-element.40), channel_id=1, source_target_pairs={{1,0},{2,1},{3,2},{4,3},{5,4},{6,5},{7,6},{8,7},{9,8},{10,9},{11,1... | collective-permute-start | bytes 294920 | tf_op jit(solution)/shard_map/ppermute | solution.py:17
  116.3 9.1 %collective-permute-start.8 = (f32[192,128]{1,0:T(8,128)S(1)}, f32[192,128]{1,0:T(8,128)S(1)}, u32[]{:S(2)}, u32[]{:S(2)}) collective-permute-start(f32[192,128]{1,0:T(8,128)S(1)} %get-tuple-element.41), channel_id=1, source_target_pairs={{0,1},{1,2},{2,3},{3,4},{4,5},{5,6},{6,7},{7,8},{8,9},{9,10},{10,1... | collective-permute-start | bytes 294920 | tf_op jit(solution)/shard_map/ppermute | solution.py:17
  118.8 54.1 %collective-permute-start.11 = (f32[192,16]{0,1:T(8,128)S(1)}, f32[192,16]{0,1:T(8,128)S(1)}, u32[]{:S(2)}, u32[]{:S(2)}) collective-permute-start(f32[192,16]{0,1:T(8,128)S(1)} %get-tuple-element.58), channel_id=1, source_target_pairs={{0,1},{1,2},{2,3},{3,4},{4,5},{5,6},{6,7},{7,8},{8,9},{9,10},{10,1... | collective-permute-start | bytes 36872 | tf_op jit(solution)/shard_map/ppermute | solution.py:17
  121.1 51.8 %collective-permute-start.10 = (f32[192,16]{0,1:T(8,128)S(1)}, f32[192,16]{0,1:T(8,128)S(1)}, u32[]{:S(2)}, u32[]{:S(2)}) collective-permute-start(f32[192,16]{0,1:T(8,128)S(1)} %get-tuple-element.55), channel_id=1, source_target_pairs={{0,16},{16,32},{32,48},{48,64},{64,80},{80,96},{96,112},{112,128},... | collective-permute-start | bytes 36872 | tf_op jit(solution)/shard_map/ppermute | solution.py:17
  184.2 58.3 %copy-start.4 = (f32[192,128]{1,0:T(8,128)S(1)}, f32[192,128]{1,0:T(8,128)}, u32[]{:S(2)}) copy-start(f32[192,128]{1,0:T(8,128)} %copy-done.3) | copy-start | bytes 294916
  184.2 58.2 %copy-start.6 = (f32[192,128]{1,0:T(8,128)S(1)}, f32[192,128]{1,0:T(8,128)}, u32[]{:S(2)}) copy-start(f32[192,128]{1,0:T(8,128)} %copy-done.5) | copy-start | bytes 294916
  184.3 8.5 %collective-permute-start.14 = (f32[192,128]{1,0:T(8,128)S(1)}, f32[192,128]{1,0:T(8,128)S(1)}, u32[]{:S(2)}, u32[]{:S(2)}) collective-permute-start(f32[192,128]{1,0:T(8,128)S(1)} %get-tuple-element.21), channel_id=1, source_target_pairs={{0,16},{16,32},{32,48},{48,64},{64,80},{80,96},{96,112},{112,128},... | collective-permute-start | bytes 294920 | tf_op jit(solution)/shard_map/ppermute | solution.py:17
  185.7 7.0 %collective-permute-start.12 = (f32[192,128]{1,0:T(8,128)S(1)}, f32[192,128]{1,0:T(8,128)S(1)}, u32[]{:S(2)}, u32[]{:S(2)}) collective-permute-start(f32[192,128]{1,0:T(8,128)S(1)} %get-tuple-element.24), channel_id=1, source_target_pairs={{16,0},{32,16},{48,32},{64,48},{80,64},{96,80},{112,96},{128,112},... | collective-permute-start | bytes 294920 | tf_op jit(solution)/shard_map/ppermute | solution.py:17
  187.0 5.9 %collective-permute-start.13 = (f32[192,128]{1,0:T(8,128)S(1)}, f32[192,128]{1,0:T(8,128)S(1)}, u32[]{:S(2)}, u32[]{:S(2)}) collective-permute-start(f32[192,128]{1,0:T(8,128)S(1)} %get-tuple-element.22), channel_id=1, source_target_pairs={{1,0},{2,1},{3,2},{4,3},{5,4},{6,5},{7,6},{8,7},{9,8},{10,9},{11,1... | collective-permute-start | bytes 294920 | tf_op jit(solution)/shard_map/ppermute | solution.py:17
  189.4 4.8 %collective-permute-start.15 = (f32[192,128]{1,0:T(8,128)S(1)}, f32[192,128]{1,0:T(8,128)S(1)}, u32[]{:S(2)}, u32[]{:S(2)}) collective-permute-start(f32[192,128]{1,0:T(8,128)S(1)} %get-tuple-element.23), channel_id=1, source_target_pairs={{0,1},{1,2},{2,3},{3,4},{4,5},{5,6},{6,7},{7,8},{8,9},{9,10},{10,1... | collective-permute-start | bytes 294920 | tf_op jit(solution)/shard_map/ppermute | solution.py:17
  194.4 48.2 %copy-start.7 = (f32[1,1,192,128]{3,2,1,0:T(8,128)S(1)}, f32[1,1,192,128]{3,2,1,0:T(8,128)}, u32[]{:S(2)}) copy-start(f32[1,1,192,128]{3,2,1,0:T(8,128)} %get-tuple-element.27) | copy-start | bytes 294916
  194.4 48.2 %copy-start.8 = (f32[1,1,192,128]{3,2,1,0:T(8,128)S(1)}, f32[1,1,192,128]{3,2,1,0:T(8,128)}, u32[]{:S(2)}) copy-start(f32[1,1,192,128]{3,2,1,0:T(8,128)} %get-tuple-element.29) | copy-start | bytes 294916
  (25 other events, 344.0 us)
